TPU v7x, 32 devices: a whole 2x2x4 slice. The times are simulated.
32 devices in a mesh: cols: 8 (over z, x), trc: 4 (over y, core).
Axes of the slice: x: 2, y: 2, z: 4, core: 2. Of those that a mesh axis runs over, the one named last changes fastest.
Arguments:
- tracers_src: bfloat16 [28, 127, 16384], P(None, None, ('cols', 'trc')), may hold values from -1 to 2
- layer_dp: float32 [127, 16384], P(None, ('cols', 'trc')), may hold values from 0.3 to 3
- cut_frac: float32 [71, 16384], P(None, ('cols', 'trc')), may hold values from 0.05 to 0.95
- level_bounds: int32 [2, 72, 16384], P(None, None, ('cols', 'trc')), may hold values from 0 to 126, as said below
Outputs:
- remapped_tracers: bfloat16 [28, 72, 16384], P('trc', None, 'cols')
- burden: float32 [28], P('trc')
Inputs may be any that keep to these rules, and one draw needn't show every extreme that they name: level_bounds[0, 0, c] = 0, level_bounds[1, 71, c] = 126, level_bounds[1, t, c] = level_bounds[0, t + 1, c], and level_bounds[0, t, c] rises strictly with t in every column.
All inputs are finite; a program needn't handle non-finite values.
Results may differ from a plain program's by a relative error of at most 0.0005.
Values may be sent and summed in bfloat16 or wider, within the bound.
A program may use at most 64 MiB of HBM per device.

v0:
```python
import jax
import jax.numpy as jnp
from jax import lax
from jax.sharding import PartitionSpec as P


def remap_block(tracers, layer_dp, cut_frac, bounds):
    columns = layer_dp.shape[1]
    tracer_count = tracers.shape[0]
    layers = layer_dp.shape[0]
    inner_first = bounds[0][1:]
    layer_index = lax.broadcasted_iota(jnp.int32, (1, layers, 1), 1)
    below = (layer_index < inner_first[:, None, :]).astype(jnp.float32)
    inside = (layer_index == inner_first[:, None, :]).astype(jnp.float32)
    intersection = below + cut_frac[:, None, :] * inside
    column_dp = jnp.sum(layer_dp, axis=0, keepdims=True)
    inner_edges = jnp.sum(intersection * layer_dp[None], axis=1)
    targets = jnp.concatenate(
        [jnp.zeros((1, columns), jnp.float32), inner_edges, column_dp], axis=0
    )
    layer_mass = tracers.astype(jnp.float32) * layer_dp[None]
    column_mass = jnp.sum(layer_mass, axis=1)
    inner_mass = jnp.einsum(
        "jsc,qsc->qjc", intersection, layer_mass, precision=lax.Precision.HIGHEST
    )
    edge_mass = jnp.concatenate(
        [jnp.zeros((tracer_count, 1, columns), jnp.float32), inner_mass, column_mass[:, None]],
        axis=1,
    )
    remapped = edge_mass[:, 1:] - edge_mass[:, :-1]
    return (remapped, targets[1:] - targets[:-1], column_mass)


def area_of(first_col, count, total_cols):
    position = first_col + lax.broadcasted_iota(jnp.int32, (count,), 0)
    return 1.0 + 2.0 * position.astype(jnp.float32) / total_cols


def remap_columns(tracers, layer_dp, cut_frac, bounds, start_col, total_cols):
    columns = layer_dp.shape[1]
    block_cols = 128
    tracer_count = tracers.shape[0]
    levels = bounds.shape[1]

    def loop_step(block_index, totals):
        remapped, target_dp, before_part = totals
        offset = block_index * block_cols

        def window(values_in):
            return lax.dynamic_slice_in_dim(values_in, offset, block_cols, values_in.ndim - 1)

        block_mass, block_dp, column_mass = remap_block(
            window(tracers), window(layer_dp), window(cut_frac), window(bounds)
        )
        cell_area = area_of(start_col + offset, block_cols, total_cols)
        before_part = before_part + jnp.sum(column_mass * cell_area[None], axis=1)
        remapped = lax.dynamic_update_slice_in_dim(remapped, block_mass, offset, 2)
        target_dp = lax.dynamic_update_slice_in_dim(target_dp, block_dp, offset, 1)
        return (remapped, target_dp, before_part)

    initial = (
        jnp.zeros((tracer_count, levels, columns), jnp.float32),
        jnp.zeros((levels, columns), jnp.float32),
        jnp.zeros((tracer_count,), jnp.float32),
    )
    return lax.fori_loop(0, columns // block_cols, loop_step, initial)


def burden_terms(remapped, target_dp, start_col, total_cols):
    positive = jnp.maximum(remapped / target_dp[None], 0.0)
    cell_area = area_of(start_col, target_dp.shape[1], total_cols)
    after_part = jnp.sum(positive * target_dp[None] * cell_area[None, None], axis=(1, 2))
    return (positive, after_part)


def per_device(tracers_src, layer_dp, cut_frac, level_bounds):
    groups = lax.axis_size("trc")
    col_dev = layer_dp.shape[1]
    total_cols = col_dev * lax.axis_size("cols") * groups
    norm_scale = 1.0 / (total_cols * layer_dp.shape[0])
    start_col = (lax.axis_index("cols") * groups + lax.axis_index("trc")) * col_dev
    remapped, target_dp, before_part = remap_columns(
        tracers_src, layer_dp, cut_frac, level_bounds, start_col, total_cols
    )
    positive, after_part = burden_terms(remapped, target_dp, start_col, total_cols)
    before_sum, after_sum = lax.psum((before_part, after_part), ("cols", "trc"))
    burden_full = before_sum * norm_scale
    fix_ratio = burden_full / (after_sum * norm_scale)
    local_result = (positive * fix_ratio[:, None, None]).astype(jnp.bfloat16)
    result = lax.all_to_all(local_result, "trc", split_axis=0, concat_axis=2, tiled=True)
    per_group = burden_full.shape[0] // groups
    burden = lax.dynamic_slice_in_dim(burden_full, lax.axis_index("trc") * per_group, per_group)
    return (result, burden)


def solution(mesh):
    in_specs = (
        P(None, None, ("cols", "trc")),
        P(None, ("cols", "trc")),
        P(None, ("cols", "trc")),
        P(None, None, ("cols", "trc")),
    )
    out_specs = (P("trc", None, "cols"), P("trc"))
    return jax.shard_map(
        per_device, mesh=mesh, in_specs=in_specs, out_specs=out_specs, check_vma=False
    )
```

profile of v0, /device:TPU:0, one launch (start us, length us, event | category | flops | bytes accessed | tf_op | source)
XLA Modules:
  0.0 213.0 jit_solution(663336179255159050)
XLA Ops:
  0.6 0.6 multiply_add_fusion.1
  1.2 2.5 %broadcast.87.clone2 = f32[28,72,512]{2,1,0:T(8,128)} broadcast(f32[]{:T(128)} %constant.106.clone.1), dimensions={} | broadcast | bytes 4128772 | tf_op jit(solution)/shard_map/broadcast.15
  3.7 129.4 %while.20 = (s32[]{:T(128)}, f32[28,72,512]{2,1,0:T(8,128)}, f32[72,512]{1,0:T(8,128)S(1)}, f32[28]{0:T(128)S(1)}, bf16[28,127,512]{2,1,0:T(8,128)(2,1)}, /*inde...) while((s32[]{:T(128)}, f32[28,72,512]{2,1,0:T(8,128)}, ...), condition=%wide.region_5.0_spmd.clone, body=%wide.region_0.0_spmd.clone.sunk | while | flops 404474784 | bytes 13883509 | solution.py:66
  3.7 0.8 constant_dynamic-slice_fusion.10
  4.7 0.8 constant_dynamic-slice_fusion.9
  5.5 0.9 fusion.14
  6.5 0.1 copy.79
  6.6 5.5 %multiply_reduce_fusion.5 = f32[71,128]{0,1:T(8,128)S(1)} fusion(f32[127,128]{0,1:T(8,128)S(1)} %copy.74, f32[71,128]{0,1:T(8,128)S(1)} %copy.76, s32[71,128]{0,1:T(8,128)S(1)} %bitcast.20), kind=kLoop, calls=%fused_computation.clone.1 | loop fusion | flops 8070144 | bytes 174080 | tf_op jit(solution)/shard_map/while/body/eval_jaxpr/reduce_sum | solution.py:17
  12.3 1.2 constant_dynamic-slice_fusion.8
  13.5 1.2 copy.73
  14.7 0.6 fusion.15
  15.5 0.5 copy-done
  16.0 10.8 %fusion.16 = f32[28,71,128]{1,0,2:T(8,128)} fusion(f32[71,128]{0,1:T(8,128)S(1)} %copy.76, s32[71,128]{0,1:T(8,128)S(1)} %bitcast.21, bf16[28,127,128]{1,0,2:T(8,128)(2,1)S(1)} %copy.73, f32[127,128]{0,1:T(8,128)S(1)} %copy.74), kind=kOutput, calls=%fused_computation.11.clone.1 | convolution fusion | flops 394484352 | bytes 2065920 | tf_op jit(solution)/shard_map/while/body/eval_jaxpr/jsc,qsc->qjc/dot_general | solution.py:23
  26.7 0.9 copy.75
  27.7 4.7 %maximum_subtract_fusion.4 = f32[28,72,128]{1,0,2:T(8,128)} fusion(f32[28,1,128]{1,0,2:T(8,128)S(1)} %copy.75, f32[28,71,128]{1,0,2:T(8,128)} %fusion.16), kind=kLoop, calls=%fused_computation.8.clone.1 | loop fusion | flops 516096 | bytes 2064384 | tf_op jit(solution)/shard_map/while/body/eval_jaxpr/sub | solution.py:30
  32.4 2.5 %copy.78 = f32[28,72,128]{2,1,0:T(8,128)S(1)} copy(f32[28,72,128]{1,0,2:T(8,128)} %maximum_subtract_fusion.4) | data formatting | bytes 2064384 | tf_op jit(solution)/shard_map/while/body/eval_jaxpr/dynamic_update_slice | solution.py:57
  34.9 1.1 constant_dynamic-update-slice_fusion.4
  36.1 0.8 constant_dynamic-slice_fusion.10
  37.0 0.8 constant_dynamic-slice_fusion.9
  37.9 0.9 fusion.14
  38.9 0.1 copy.79
  39.0 5.5 %multiply_reduce_fusion.5 = f32[71,128]{0,1:T(8,128)S(1)} fusion(f32[127,128]{0,1:T(8,128)S(1)} %copy.74, f32[71,128]{0,1:T(8,128)S(1)} %copy.76, s32[71,128]{0,1:T(8,128)S(1)} %bitcast.20), kind=kLoop, calls=%fused_computation.clone.1 | loop fusion | flops 8070144 | bytes 174080 | tf_op jit(solution)/shard_map/while/body/eval_jaxpr/reduce_sum | solution.py:17
  44.7 1.2 constant_dynamic-slice_fusion.8
  45.9 1.2 copy.73
  47.1 0.6 fusion.15
  47.8 0.5 copy-done
  48.3 10.8 %fusion.16 = f32[28,71,128]{1,0,2:T(8,128)} fusion(f32[71,128]{0,1:T(8,128)S(1)} %copy.76, s32[71,128]{0,1:T(8,128)S(1)} %bitcast.21, bf16[28,127,128]{1,0,2:T(8,128)(2,1)S(1)} %copy.73, f32[127,128]{0,1:T(8,128)S(1)} %copy.74), kind=kOutput, calls=%fused_computation.11.clone.1 | convolution fusion | flops 394484352 | bytes 2065920 | tf_op jit(solution)/shard_map/while/body/eval_jaxpr/jsc,qsc->qjc/dot_general | solution.py:23
  59.1 0.9 copy.75
  60.1 4.7 %maximum_subtract_fusion.4 = f32[28,72,128]{1,0,2:T(8,128)} fusion(f32[28,1,128]{1,0,2:T(8,128)S(1)} %copy.75, f32[28,71,128]{1,0,2:T(8,128)} %fusion.16), kind=kLoop, calls=%fused_computation.8.clone.1 | loop fusion | flops 516096 | bytes 2064384 | tf_op jit(solution)/shard_map/while/body/eval_jaxpr/sub | solution.py:30
  64.8 2.5 %copy.78 = f32[28,72,128]{2,1,0:T(8,128)S(1)} copy(f32[28,72,128]{1,0,2:T(8,128)} %maximum_subtract_fusion.4) | data formatting | bytes 2064384 | tf_op jit(solution)/shard_map/while/body/eval_jaxpr/dynamic_update_slice | solution.py:57
  67.3 1.1 constant_dynamic-update-slice_fusion.4
  68.4 0.8 constant_dynamic-slice_fusion.10
  69.4 0.8 constant_dynamic-slice_fusion.9
  70.3 0.9 fusion.14
  71.4 5.5 %multiply_reduce_fusion.5 = f32[71,128]{0,1:T(8,128)S(1)} fusion(f32[127,128]{0,1:T(8,128)S(1)} %copy.74, f32[71,128]{0,1:T(8,128)S(1)} %copy.76, s32[71,128]{0,1:T(8,128)S(1)} %bitcast.20), kind=kLoop, calls=%fused_computation.clone.1 | loop fusion | flops 8070144 | bytes 174080 | tf_op jit(solution)/shard_map/while/body/eval_jaxpr/reduce_sum | solution.py:17
  77.0 1.2 constant_dynamic-slice_fusion.8
  78.3 1.2 copy.73
  79.4 0.6 fusion.15
  80.2 0.5 copy-done
  80.7 10.8 %fusion.16 = f32[28,71,128]{1,0,2:T(8,128)} fusion(f32[71,128]{0,1:T(8,128)S(1)} %copy.76, s32[71,128]{0,1:T(8,128)S(1)} %bitcast.21, bf16[28,127,128]{1,0,2:T(8,128)(2,1)S(1)} %copy.73, f32[127,128]{0,1:T(8,128)S(1)} %copy.74), kind=kOutput, calls=%fused_computation.11.clone.1 | convolution fusion | flops 394484352 | bytes 2065920 | tf_op jit(solution)/shard_map/while/body/eval_jaxpr/jsc,qsc->qjc/dot_general | solution.py:23
  91.5 0.9 copy.75
  92.4 4.7 %maximum_subtract_fusion.4 = f32[28,72,128]{1,0,2:T(8,128)} fusion(f32[28,1,128]{1,0,2:T(8,128)S(1)} %copy.75, f32[28,71,128]{1,0,2:T(8,128)} %fusion.16), kind=kLoop, calls=%fused_computation.8.clone.1 | loop fusion | flops 516096 | bytes 2064384 | tf_op jit(solution)/shard_map/while/body/eval_jaxpr/sub | solution.py:30
  97.1 2.5 %copy.78 = f32[28,72,128]{2,1,0:T(8,128)S(1)} copy(f32[28,72,128]{1,0,2:T(8,128)} %maximum_subtract_fusion.4) | data formatting | bytes 2064384 | tf_op jit(solution)/shard_map/while/body/eval_jaxpr/dynamic_update_slice | solution.py:57
  99.7 1.1 constant_dynamic-update-slice_fusion.4
  100.8 0.8 constant_dynamic-slice_fusion.10
  101.7 0.8 constant_dynamic-slice_fusion.9
  102.6 0.9 fusion.14
  103.7 5.5 %multiply_reduce_fusion.5 = f32[71,128]{0,1:T(8,128)S(1)} fusion(f32[127,128]{0,1:T(8,128)S(1)} %copy.74, f32[71,128]{0,1:T(8,128)S(1)} %copy.76, s32[71,128]{0,1:T(8,128)S(1)} %bitcast.20), kind=kLoop, calls=%fused_computation.clone.1 | loop fusion | flops 8070144 | bytes 174080 | tf_op jit(solution)/shard_map/while/body/eval_jaxpr/reduce_sum | solution.py:17
  109.4 1.2 constant_dynamic-slice_fusion.8
  110.6 1.2 copy.73
  111.8 0.6 fusion.15
  112.5 0.5 copy-done
  113.1 10.8 %fusion.16 = f32[28,71,128]{1,0,2:T(8,128)} fusion(f32[71,128]{0,1:T(8,128)S(1)} %copy.76, s32[71,128]{0,1:T(8,128)S(1)} %bitcast.21, bf16[28,127,128]{1,0,2:T(8,128)(2,1)S(1)} %copy.73, f32[127,128]{0,1:T(8,128)S(1)} %copy.74), kind=kOutput, calls=%fused_computation.11.clone.1 | convolution fusion | flops 394484352 | bytes 2065920 | tf_op jit(solution)/shard_map/while/body/eval_jaxpr/jsc,qsc->qjc/dot_general | solution.py:23
  123.8 0.9 copy.75
  124.8 4.7 %maximum_subtract_fusion.4 = f32[28,72,128]{1,0,2:T(8,128)} fusion(f32[28,1,128]{1,0,2:T(8,128)S(1)} %copy.75, f32[28,71,128]{1,0,2:T(8,128)} %fusion.16), kind=kLoop, calls=%fused_computation.8.clone.1 | loop fusion | flops 516096 | bytes 2064384 | tf_op jit(solution)/shard_map/while/body/eval_jaxpr/sub | solution.py:30
  129.5 2.5 %copy.78 = f32[28,72,128]{2,1,0:T(8,128)S(1)} copy(f32[28,72,128]{1,0,2:T(8,128)} %maximum_subtract_fusion.4) | data formatting | bytes 2064384 | tf_op jit(solution)/shard_map/while/body/eval_jaxpr/dynamic_update_slice | solution.py:57
  132.0 1.1 constant_dynamic-update-slice_fusion.4
  133.1 3.1 %multiply_reduce_fusion.2 = f32[28]{0:T(128)S(1)} fusion(f32[512]{0:T(512)} %multiply_add_fusion.1, f32[72,512]{1,0:T(8,128)S(1)} %get-tuple-element.225, f32[28,72,512]{2,1,0:T(8,128)} %get-tuple-element.224), kind=kLoop, calls=%fused_computation.26 | loop fusion | flops 5160932 | bytes 4278384 | tf_op jit(solution)/shard_map/reduce_sum | solution.py:72
  136.2 42.0 %all-reduce.2 = (f32[28]{0:T(128)S(1)}, f32[28]{0:T(128)S(1)}) all-reduce(f32[28]{0:T(128)S(1)} %multiply_reduce_fusion.2, f32[28]{0:T(128)S(1)} %get-tuple-element.226), channel_id=1, replica_groups=mesh['cols'=8,'trc'=4] {'cols','trc'}, use_global_device_ids=true, to_apply=%region_8.0 | all-reduce | flops 56 | bytes 448 | tf_op jit(solution)/shard_map/psum | solution.py:86
  178.2 4.3 %multiply_convert_fusion = bf16[28,72,512]{2,1,0:T(8,128)(2,1)} fusion(f32[28]{0:T(128)S(1)} %get-tuple-element.325, f32[28,72,512]{2,1,0:T(8,128)} %get-tuple-element.224, f32[72,512]{1,0:T(8,128)S(1)} %get-tuple-element.225), kind=kLoop, calls=%fused_computation.25 | loop fusion | flops 4128768 | bytes 6340720 | tf_op jit(solution)/shard_map/convert_element_type | solution.py:89
  182.5 3.6 %all-to-all-start = ((bf16[28,72,512]{2,1,0:T(8,128)(2,1)}), bf16[28,72,512]{2,1,0:T(8,128)(2,1)S(1)}, u32[]{:S(2)}, u32[]{:S(2)}) async-start(bf16[28,72,512]{2,1,0:T(8,128)(2,1)} %multiply_convert_fusion), calls=%async_computation | async-start | bytes 4128768 | tf_op jit(solution)/shard_map/all_to_all | solution.py:90
  186.1 0.6 dynamic_slice.43
  186.7 24.7 %all-to-all-done = bf16[28,72,512]{2,1,0:T(8,128)(2,1)S(1)} async-done(((bf16[28,72,512]{2,1,0:T(8,128)(2,1)}), bf16[28,72,512]{2,1,0:T(8,128)(2,1)S(1)}, u32[]{:S(2)}, u32[]{:S(2)}) %all-to-all-start) | async-done | bytes 2064416 | tf_op jit(solution)/shard_map/all_to_all | solution.py:90
  211.4 1.6 copy.64
  (53 shorter events, 2.6 us)
Async XLA Ops:
  15.4 0.5 copy-start
  32.4 3.7 %copy-start.1 = (f32[28]{0:T(128)S(1)}, f32[28]{0:T(128)}, u32[]{:S(2)}) copy-start(f32[28]{0:T(128)} %copy-done) | copy-start | bytes 340 | tf_op jit(solution)/shard_map/while
  47.8 0.5 copy-start
  64.8 3.7 %copy-start.1 = (f32[28]{0:T(128)S(1)}, f32[28]{0:T(128)}, u32[]{:S(2)}) copy-start(f32[28]{0:T(128)} %copy-done) | copy-start | bytes 340 | tf_op jit(solution)/shard_map/while
  80.2 0.5 copy-start
  97.1 3.7 %copy-start.1 = (f32[28]{0:T(128)S(1)}, f32[28]{0:T(128)}, u32[]{:S(2)}) copy-start(f32[28]{0:T(128)} %copy-done) | copy-start | bytes 340 | tf_op jit(solution)/shard_map/while
  112.5 0.5 copy-start
  129.5 3.6 %copy-start.1 = (f32[28]{0:T(128)S(1)}, f32[28]{0:T(128)}, u32[]{:S(2)}) copy-start(f32[28]{0:T(128)} %copy-done) | copy-start | bytes 340 | tf_op jit(solution)/shard_map/while
  182.5 28.9 %all-to-all-start = ((bf16[28,72,512]{2,1,0:T(8,128)(2,1)}), bf16[28,72,512]{2,1,0:T(8,128)(2,1)S(1)}, u32[]{:S(2)}, u32[]{:S(2)}) async-start(bf16[28,72,512]{2,1,0:T(8,128)(2,1)} %multiply_convert_fusion), calls=%async_computation | async-start | bytes 4128768 | tf_op jit(solution)/shard_map/all_to_all | solution.py:90
where the time goes:
time: 214 us; the launch traced here: 213 us
  other arithmetic  55.5 us (26%)
  local copies, waits for them, and re-layouts  43.1 us (20%)
  matrix products  43.1 us (20%)
  blocking collectives  42 us (20%)
  waiting for transfers between devices  24.7 us (12%)
  starting transfers between devices  3.61 us (2%)
    dot_general x4, matrix products, remap_block(): jnp.einsum('jsc,qsc->qjc', intersection, layer_mass, precision=lax.Precis...  43.1 us
    psum x1, blocking collectives, per_device(): before_sum, after_sum = lax.psum((before_part, after_part), ('cols', 'trc'))  42 us
    all_to_all x1, waiting for transfers between devices, per_device(): lax.all_to_all(local_result, 'trc', split_axis=0, concat_axis=2, tiled=True)  24.7 us
    reduce_sum x4, other arithmetic, remap_block(): inner_edges = jnp.sum(intersection * layer_dp[None], axis=1)  21.8 us
    sub x4, other arithmetic, remap_block(): remapped = edge_mass[:, 1:] - edge_mass[:, :-1]  18.9 us
    dynamic_update_slice x8, local copies, waits for them, and re-layouts, loop_step(): remapped = lax.dynamic_update_slice_in_dim(remapped, block_mass, offset, 2)  14.6 us
    dynamic_slice x20, local copies, waits for them, and re-layouts, window(): lax.dynamic_slice_in_dim(values_in, offset, block_cols, values_in.ndim - 1)  13.5 us
  transfers between devices with their start and end apart: 1, of which 1 were waited for; matrix products, arithmetic and copies ran while one was open for 0% of the time, Pallas kernels for 0%

commit v1 on v0

v1 whole, which is shorter than its diff:
```python
import functools

import jax
import jax.numpy as jnp
from jax import lax
from jax.experimental import pallas as pl
from jax.experimental.pallas import tpu as pltpu
from jax.sharding import PartitionSpec as P

MESH = pl.DeviceIdType.MESH
F32 = jnp.float32
LANES = 128
ROWS = 8


def take_rows(values, rows):
    return jnp.take_along_axis(values, rows, axis=0, mode="promise_in_bounds")


def running_sum(pieces, row):
    result, carry = [], None
    last = jnp.full((ROWS, LANES), ROWS - 1, jnp.int32)
    for piece in pieces:
        for step in (1, 2, 4):
            piece = piece + jnp.where(row >= step, pltpu.roll(piece, step, 0), 0.0)
        total = take_rows(piece, last)
        result.append(piece if carry is None else piece + carry)
        carry = total if carry is None else carry + total
    return result


def edge_values(values, low, high, layers, levels):
    slack = layers - levels
    edges = []
    for piece in range(levels // ROWS):
        first = (piece * ROWS + 1) // ROWS
        final = min((piece * ROWS + ROWS + slack) // ROWS, len(values) - 1)
        picked = None
        for source in range(first, final + 1):
            here = take_rows(values[source], low[piece])
            picked = here if picked is None else jnp.where(high[piece] == source, here, picked)
        edges.append(picked)
    return edges


def differences(edges, row):
    result, before = [], jnp.zeros((ROWS, LANES), F32)
    for edge in edges:
        turned = pltpu.roll(edge, 1, 0)
        result.append(edge - jnp.where(row == 0, before, turned))
        before = turned
    return result


def kernel(
    cols, groups, x_ref, dp_ref, cut_ref, bounds_ref, out_ref, burden_ref,
    positive, stage, mass_rows, dp_rows, blend, target, inverse, part, packed, arrived, ratio,
    sum_send, sum_recv, move_send, move_recv, own_sem,
):
    tracers, layers, columns = x_ref.shape
    levels = bounds_ref.shape[1]
    per = tracers // groups
    devices = cols * groups
    pieces = (layers + ROWS) // ROWS
    slack = layers - levels
    c_id, g_id = lax.axis_index("cols"), lax.axis_index("trc")
    me = c_id * groups + g_id
    norm = 1.0 / (columns * devices * layers)

    barrier = pltpu.get_barrier_semaphore()
    for step in range(1, devices):
        peer = lax.rem(me + step, devices)
        pl.semaphore_signal(
            barrier, inc=1, device_id=(peer // groups, lax.rem(peer, groups)), device_id_type=MESH
        )

    row = lax.broadcasted_iota(jnp.int32, (ROWS, LANES), 0)
    lane = lax.broadcasted_iota(jnp.int32, (1, LANES), 1)
    part[...] = jnp.zeros_like(part)
    mass_rows[...] = jnp.zeros_like(mass_rows)
    dp_rows[...] = jnp.zeros_like(dp_rows)

    def column_block(block, _):
        offset = pl.multiple_of(block * LANES, LANES)
        cs = pl.ds(offset, LANES)
        target[0 : levels - 1] = bounds_ref[0, 1:, cs]
        target[levels - 1 : levels] = jnp.full((1, LANES), layers, jnp.int32)
        dp_rows[0:layers] = dp_ref[:, cs]
        for piece in range(pieces):
            first = max(1, piece * ROWS - slack)
            final = min(levels - 1, piece * ROWS + ROWS - 1)
            weight = jnp.full((ROWS, LANES), -1.0, F32)
            for j in range(first, final + 1):
                found = target[j - 1 : j] == row + piece * ROWS
                weight = jnp.where(found, cut_ref[j - 1 : j, cs] - 1.0, weight)
            blend[piece] = weight
        bounds = [target[p * ROWS : (p + 1) * ROWS] for p in range(levels // ROWS)]
        low = [jnp.bitwise_and(b, ROWS - 1) for b in bounds]
        high = [lax.shift_right_logical(b, 3) for b in bounds]

        def remap(mass):
            sums = running_sum(mass, row)
            values = [s + blend[p] * m for p, (s, m) in enumerate(zip(sums, mass))]
            edges = edge_values(values, low, high, layers, levels)
            return differences(edges, row), values[-1]

        thickness, _ = remap([dp_rows[p * ROWS : (p + 1) * ROWS] for p in range(pieces)])
        for p, t in enumerate(thickness):
            inverse[p] = 1.0 / t
        area = 1.0 + 2.0 * (lane + offset + me * columns).astype(F32) / (columns * devices)

        def tracer(q, _):
            mass_rows[0:layers] = x_ref[q, :, cs].astype(F32)
            mass = [
                mass_rows[p * ROWS : (p + 1) * ROWS] * dp_rows[p * ROWS : (p + 1) * ROWS]
                for p in range(pieces)
            ]
            moved, top = remap(mass)
            kept = jnp.zeros((ROWS, LANES), F32)
            for p, m in enumerate(moved):
                m = jnp.maximum(m, 0.0)
                kept = kept + m
                positive[q, p * ROWS : (p + 1) * ROWS, cs] = m * inverse[p]
            before = top[layers % ROWS : layers % ROWS + 1]
            part[0, pl.ds(q, 1), :] += before * area
            part[1, pl.ds(q, 1), :] += jnp.sum(kept, axis=0, keepdims=True) * area
            return 0

        return lax.fori_loop(0, tracers, tracer, 0)

    lax.fori_loop(0, columns // LANES, column_block, 0)

    t_row = lax.broadcasted_iota(jnp.int32, (tracers, LANES), 0)
    t_lane = lax.broadcasted_iota(jnp.int32, (tracers, LANES), 1)

    def to_row(values, shift):
        return jnp.sum(jnp.where(t_row == t_lane + shift, values, 0.0), axis=0, keepdims=True)

    def to_column(values):
        return jnp.sum(jnp.where(t_row == t_lane, values, 0.0), axis=1, keepdims=True)

    packed[...] = jnp.zeros_like(packed)
    for kind in range(2):
        packed[kind : kind + 1] = to_row(jnp.sum(part[kind], axis=1, keepdims=True), 0)
    arrived[pl.ds(me, 1)] = packed[...][None]
    pl.semaphore_wait(barrier, devices - 1)
    sums = []
    for step in range(1, devices):
        peer = lax.rem(me + step, devices)
        copy = pltpu.make_async_remote_copy(
            src_ref=packed, dst_ref=arrived.at[me], send_sem=sum_send.at[step - 1], recv_sem=sum_recv.at[step - 1],
            device_id=(peer // groups, lax.rem(peer, groups)), device_id_type=MESH,
        )
        copy.start()
        sums.append(copy)
    for copy in sums:
        copy.wait()
    total = jnp.sum(arrived[...], axis=0) * norm
    before = to_column(total[0:1])
    after = to_column(total[1:2])
    ratio[...] = jnp.broadcast_to(before / after, (tracers, LANES))
    burden_ref[...] = to_row(before, g_id * per)[:, 0:per]

    place = pl.ds(pl.multiple_of(g_id * columns, LANES), columns)

    def fill(h, q):
        t = h * per + q
        scale = jnp.tile(ratio[pl.ds(t, 1), :], (1, columns // LANES))
        stage[h, q] = (positive[t] * scale).astype(jnp.bfloat16)

    order = sorted(range(1, groups), reverse=True)
    copies = []
    for q in range(per):
        for k in order:
            h = jnp.bitwise_xor(g_id, k)
            fill(h, q)
            copy = pltpu.make_async_remote_copy(
                src_ref=stage.at[h, q], dst_ref=out_ref.at[q, :, place],
                send_sem=move_send.at[q, k - 1], recv_sem=move_recv.at[q, k - 1],
                device_id=(c_id, h), device_id_type=MESH,
            )
            copy.start()
            copies.append(copy)
    for q in range(per):
        fill(g_id, q)
    own = pltpu.make_async_copy(stage.at[g_id], out_ref.at[:, :, place], own_sem)
    own.start()
    own.wait()
    for copy in copies:
        copy.wait()


def per_device(cols, groups, tracers_src, layer_dp, cut_frac, level_bounds):
    tracers, layers, columns = tracers_src.shape
    levels = level_bounds.shape[1]
    per = tracers // groups
    padded = -(-(layers + 1) // ROWS) * ROWS
    vmem = pl.BlockSpec(memory_space=pltpu.VMEM)
    result, burden = pl.pallas_call(
        functools.partial(kernel, cols, groups),
        out_shape=(
            jax.ShapeDtypeStruct((per, levels, columns * groups), jnp.bfloat16),
            jax.ShapeDtypeStruct((1, per), F32),
        ),
        in_specs=[vmem] * 4,
        out_specs=(pl.BlockSpec(memory_space=pl.ANY), vmem),
        scratch_shapes=[
            pltpu.VMEM((tracers, levels, columns), F32),
            pltpu.VMEM((groups, per, levels, columns), jnp.bfloat16),
            pltpu.VMEM((padded, LANES), F32),
            pltpu.VMEM((padded, LANES), F32),
            pltpu.VMEM((padded // ROWS, ROWS, LANES), F32),
            pltpu.VMEM((levels, LANES), jnp.int32),
            pltpu.VMEM((levels // ROWS, ROWS, LANES), F32),
            pltpu.VMEM((2, tracers, LANES), F32),
            pltpu.VMEM((ROWS, LANES), F32),
            pltpu.VMEM((cols * groups, ROWS, LANES), F32),
            pltpu.VMEM((tracers, LANES), F32),
            pltpu.SemaphoreType.DMA((cols * groups - 1,)),
            pltpu.SemaphoreType.DMA((cols * groups - 1,)),
            pltpu.SemaphoreType.DMA((per, groups - 1)),
            pltpu.SemaphoreType.DMA((per, groups - 1)),
            pltpu.SemaphoreType.DMA,
        ],
        compiler_params=pltpu.CompilerParams(
            collective_id=0, has_side_effects=True, vmem_limit_bytes=60 * 1024 * 1024
        ),
        name="remap_fix_exchange",
    )(tracers_src, layer_dp, cut_frac, level_bounds)
    return result, burden.reshape(per)


def solution(mesh):
    spread = ("cols", "trc")
    in_specs = (P(None, None, spread), P(None, spread), P(None, spread), P(None, None, spread))
    out_specs = (P("trc", None, "cols"), P("trc"))
    return jax.shard_map(
        functools.partial(per_device, mesh.shape["cols"], mesh.shape["trc"]),
        mesh=mesh, in_specs=in_specs, out_specs=out_specs, check_vma=False,
    )
```

time: 214 us -> 52.1 us (0.24)
  other arithmetic: 55.5 us -> 0 us
  Pallas kernels: 0 us -> 47.6 us
  matrix products: 43.1 us -> 0 us
  blocking collectives: 42 us -> 0 us
  local copies, waits for them, and re-layouts: 43.1 us -> 3.65 us
  waiting for transfers between devices: 24.7 us -> 0 us
  starting transfers between devices: 3.61 us -> 0 us
    pallas_call x0 -> x1, Pallas kernels: none -> 47.6 us  [per_device(): pl.pallas_call(functools.partial(kernel, cols, groups), out_shape=(jax.Sh...]
    dot_general x4 -> x0, matrix products: 43.1 us -> none  [remap_block(): jnp.einsum('jsc,qsc->qjc', intersection, layer_mass, precision=lax.Precis...]
    psum x1 -> x0, blocking collectives: 42 us -> none  [per_device(): before_sum, after_sum = lax.psum((before_part, after_part), ('cols', 'trc'))]
    reduce_sum x17 -> x0, other arithmetic: 31.3 us -> none  [the longest x4 21.8 us: remap_block(): inner_edges = jnp.sum(intersection * layer_dp[None], axis=1)]
    all_to_all x1 -> x0, waiting for transfers between devices: 24.7 us -> none  [per_device(): lax.all_to_all(local_result, 'trc', split_axis=0, concat_axis=2, tiled=True)]
    sub x8 -> x0, other arithmetic: 19.3 us -> none  [the longest x4 18.9 us: remap_block(): remapped = edge_mass[:, 1:] - edge_mass[:, :-1]]
    dynamic_update_slice x16 -> x0, local copies, waits for them, and re-layouts: 14.9 us -> none  [the longest x8 14.6 us: loop_step(): remapped = lax.dynamic_update_slice_in_dim(remapped, block_mass, offset, 2)]
    dynamic_slice x21 -> x0, local copies, waits for them, and re-layouts: 14.1 us -> none  [the longest x20 13.5 us: window(): lax.dynamic_slice_in_dim(values_in, offset, block_cols, values_in.ndim - 1)]
  transfers between devices with their start and end apart: 1 -> 0, of which waited for: 1 -> 0; matrix products, arithmetic and copies ran while one was open for 0% -> 0% of each run, Pallas kernels for 0% -> 0%
where the time goes in v1:
time: 52.1 us; the launch traced here: 51.9 us
  Pallas kernels  47.6 us (91%)
  local copies, waits for them, and re-layouts  3.65 us (7%)
  between operations  0.65 us (1%)
    pallas_call x1, Pallas kernels, per_device(): pl.pallas_call(functools.partial(kernel, cols, groups), out_shape=(jax.Sh...  47.6 us
    unnamed x4, local copies, waits for them, and re-layouts  3.65 us

profile of v1, /device:TPU:0, one launch (start us, length us, event | category | flops | bytes accessed | tf_op | source)
XLA Modules:
  0.0 51.9 jit_solution(9156348000959229536)
XLA Ops:
  0.6 47.6 %remap_fix_exchange.1 = (bf16[7,72,2048]{2,1,0:T(8,128)(2,1)}, f32[1,7]{1,0:T(1,128)}) custom-call(bf16[28,127,512]{2,1,0:T(8,128)(2,1)} %x_ref.1, f32[127,512]{1,0:T(8,128)} %dp_ref.1, f32[71,512]{1,0:T(8,128)} %cut_ref.1, s32[2,72,512]{2,1,0:T(8,128)} %bounds_ref.1), custom_call_target="tpu_custom_call" | custom-call | tf_op jit(solution)/shard_map/remap_fix_exchange/pallas_call | solution.py:199
  48.3 0.0 copy-start
  48.3 3.1 %copy.8 = bf16[7,72,2048]{2,1,0:T(8,128)(2,1)} copy(bf16[7,72,2048]{2,1,0:T(8,128)(2,1)} %get-tuple-element.8) | data formatting | bytes 4128768
  51.4 0.0 copy-done
  51.4 0.5 copy.9
Async XLA Ops:
  48.3 3.1 %copy-start = (f32[1,7]{1,0:T(1,128)S(1)}, f32[1,7]{1,0:T(1,128)}, u32[]{:S(2)}) copy-start(f32[1,7]{1,0:T(1,128)} %get-tuple-element.5) | copy-start | bytes 88

commit v2 on v1

--- a/solution.py
+++ b/solution.py
@@ -11,6 +11,7 @@
 F32 = jnp.float32
 LANES = 128
 ROWS = 8
+EARLY = 2
 
 
 def take_rows(values, rows):
@@ -55,7 +56,7 @@
 def kernel(
     cols, groups, x_ref, dp_ref, cut_ref, bounds_ref, out_ref, burden_ref,
     positive, stage, mass_rows, dp_rows, blend, target, inverse, part, packed, arrived, ratio,
-    sum_send, sum_recv, move_send, move_recv, own_sem,
+    early, landed, sum_send, sum_recv, move_send, move_recv, early_send, early_recv, own_sem,
 ):
     tracers, layers, columns = x_ref.shape
     levels = bounds_ref.shape[1]
@@ -79,6 +80,20 @@
     part[...] = jnp.zeros_like(part)
     mass_rows[...] = jnp.zeros_like(mass_rows)
     dp_rows[...] = jnp.zeros_like(dp_rows)
+
+    order = sorted(range(1, groups), reverse=True)
+
+    def early_copies(block, cs):
+        copies = []
+        for e in range(EARLY):
+            for k in order:
+                h = jnp.bitwise_xor(g_id, k)
+                copies.append(pltpu.make_async_remote_copy(
+                    src_ref=positive.at[h * per + e, :, cs], dst_ref=early.at[k - 1, e, :, cs],
+                    send_sem=early_send.at[block, e, k - 1], recv_sem=early_recv.at[block, e, k - 1],
+                    device_id=(c_id, h), device_id_type=MESH,
+                ))
+        return copies
 
     def column_block(block, _):
         offset = pl.multiple_of(block * LANES, LANES)
@@ -109,7 +124,10 @@
             inverse[p] = 1.0 / t
         area = 1.0 + 2.0 * (lane + offset + me * columns).astype(F32) / (columns * devices)
 
-        def tracer(q, _):
+        def tracer(step, _):
+            rest = step - groups * EARLY
+            late = (rest // (per - EARLY)) * per + EARLY + lax.rem(rest, per - EARLY)
+            q = jnp.where(rest < 0, (step // EARLY) * per + lax.rem(step, EARLY), late)
             mass_rows[0:layers] = x_ref[q, :, cs].astype(F32)
             mass = [
                 mass_rows[p * ROWS : (p + 1) * ROWS] * dp_rows[p * ROWS : (p + 1) * ROWS]
@@ -124,6 +142,16 @@
             before = top[layers % ROWS : layers % ROWS + 1]
             part[0, pl.ds(q, 1), :] += before * area
             part[1, pl.ds(q, 1), :] += jnp.sum(kept, axis=0, keepdims=True) * area
+
+            @pl.when(rest == 0)
+            def _():
+                @pl.when(block == 0)
+                def _():
+                    pl.semaphore_wait(barrier, devices - 1)
+
+                for copy in early_copies(block, cs):
+                    copy.start()
+
             return 0
 
         return lax.fori_loop(0, tracers, tracer, 0)
@@ -143,7 +171,6 @@
     for kind in range(2):
         packed[kind : kind + 1] = to_row(jnp.sum(part[kind], axis=1, keepdims=True), 0)
     arrived[pl.ds(me, 1)] = packed[...][None]
-    pl.semaphore_wait(barrier, devices - 1)
     sums = []
     for step in range(1, devices):
         peer = lax.rem(me + step, devices)
@@ -161,32 +188,44 @@
     ratio[...] = jnp.broadcast_to(before / after, (tracers, LANES))
     burden_ref[...] = to_row(before, g_id * per)[:, 0:per]
 
-    place = pl.ds(pl.multiple_of(g_id * columns, LANES), columns)
-
-    def fill(h, q):
-        t = h * per + q
+    def place(h):
+        return pl.ds(pl.multiple_of(h * columns, LANES), columns)
+
+    def scaled(values, t):
         scale = jnp.tile(ratio[pl.ds(t, 1), :], (1, columns // LANES))
-        stage[h, q] = (positive[t] * scale).astype(jnp.bfloat16)
-
-    order = sorted(range(1, groups), reverse=True)
+        return (values * scale).astype(jnp.bfloat16)
+
     copies = []
-    for q in range(per):
+    for q in range(EARLY, per):
         for k in order:
             h = jnp.bitwise_xor(g_id, k)
-            fill(h, q)
+            stage[h, q] = scaled(positive[h * per + q], h * per + q)
             copy = pltpu.make_async_remote_copy(
-                src_ref=stage.at[h, q], dst_ref=out_ref.at[q, :, place],
+                src_ref=stage.at[h, q], dst_ref=out_ref.at[q, :, place(g_id)],
                 send_sem=move_send.at[q, k - 1], recv_sem=move_recv.at[q, k - 1],
                 device_id=(c_id, h), device_id_type=MESH,
             )
             copy.start()
             copies.append(copy)
     for q in range(per):
-        fill(g_id, q)
-    own = pltpu.make_async_copy(stage.at[g_id], out_ref.at[:, :, place], own_sem)
+        stage[g_id, q] = scaled(positive[g_id * per + q], g_id * per + q)
+    own = pltpu.make_async_copy(stage.at[g_id], out_ref.at[:, :, place(g_id)], own_sem.at[0])
     own.start()
-    own.wait()
-    for copy in copies:
+    for block in range(columns // LANES):
+        for copy in early_copies(block, pl.ds(block * LANES, LANES)):
+            copy.wait()
+    local = [own]
+    for k in order:
+        for e in range(EARLY):
+            landed[k - 1, e] = scaled(early[k - 1, e], g_id * per + e)
+        copy = pltpu.make_async_copy(
+            landed.at[k - 1],
+            out_ref.at[0:EARLY, :, place(jnp.bitwise_xor(g_id, k))],
+            own_sem.at[k],
+        )
+        copy.start()
+        local.append(copy)
+    for copy in local + copies:
         copy.wait()
 
 
@@ -213,14 +252,18 @@
             pltpu.VMEM((levels, LANES), jnp.int32),
             pltpu.VMEM((levels // ROWS, ROWS, LANES), F32),
             pltpu.VMEM((2, tracers, LANES), F32),
-            pltpu.VMEM((ROWS, LANES), F32),
-            pltpu.VMEM((cols * groups, ROWS, LANES), F32),
+            pltpu.VMEM((2, LANES), F32),
+            pltpu.VMEM((cols * groups, 2, LANES), F32),
             pltpu.VMEM((tracers, LANES), F32),
+            pltpu.VMEM((groups - 1, EARLY, levels, columns), F32),
+            pltpu.VMEM((groups - 1, EARLY, levels, columns), jnp.bfloat16),
             pltpu.SemaphoreType.DMA((cols * groups - 1,)),
             pltpu.SemaphoreType.DMA((cols * groups - 1,)),
             pltpu.SemaphoreType.DMA((per, groups - 1)),
             pltpu.SemaphoreType.DMA((per, groups - 1)),
-            pltpu.SemaphoreType.DMA,
+            pltpu.SemaphoreType.DMA((columns // LANES, EARLY, groups - 1)),
+            pltpu.SemaphoreType.DMA((columns // LANES, EARLY, groups - 1)),
+            pltpu.SemaphoreType.DMA((groups,)),
         ],
         compiler_params=pltpu.CompilerParams(
             collective_id=0, has_side_effects=True, vmem_limit_bytes=60 * 1024 * 1024

time: 52.1 us -> 48.7 us (0.935)
  Pallas kernels: 47.6 us -> 44.2 us
    pallas_call x1, Pallas kernels: 47.6 us -> 44.2 us  [per_device(): pl.pallas_call(functools.partial(kernel, cols, groups), out_shape=(jax.Sh...]
where the time goes in v2:
time: 48.7 us; the launch traced here: 48.5 us
  Pallas kernels  44.2 us (91%)
  local copies, waits for them, and re-layouts  3.65 us (7%)
  between operations  0.65 us (1%)
    pallas_call x1, Pallas kernels, per_device(): pl.pallas_call(functools.partial(kernel, cols, groups), out_shape=(jax.Sh...  44.2 us
    unnamed x4, local copies, waits for them, and re-layouts  3.65 us

profile of v2, /device:TPU:0, one launch (start us, length us, event | category | flops | bytes accessed | tf_op | source)
XLA Modules:
  0.0 48.5 jit_solution(17326216769962934741)
XLA Ops:
  0.6 44.2 %remap_fix_exchange.1 = (bf16[7,72,2048]{2,1,0:T(8,128)(2,1)}, f32[1,7]{1,0:T(1,128)}) custom-call(bf16[28,127,512]{2,1,0:T(8,128)(2,1)} %x_ref.1, f32[127,512]{1,0:T(8,128)} %dp_ref.1, f32[71,512]{1,0:T(8,128)} %cut_ref.1, s32[2,72,512]{2,1,0:T(8,128)} %bounds_ref.1), custom_call_target="tpu_custom_call" | custom-call | tf_op jit(solution)/shard_map/remap_fix_exchange/pallas_call | solution.py:238
  44.9 0.0 copy-start
  44.9 3.1 %copy.8 = bf16[7,72,2048]{2,1,0:T(8,128)(2,1)} copy(bf16[7,72,2048]{2,1,0:T(8,128)(2,1)} %get-tuple-element.8) | data formatting | bytes 4128768
  48.0 0.0 copy-done
  48.0 0.5 %copy.9 = f32[7]{0:T(128)} copy(f32[7]{0:T(128)S(1)} %bitcast.1) | data formatting | bytes 56
Async XLA Ops:
  44.9 3.1 %copy-start = (f32[1,7]{1,0:T(1,128)S(1)}, f32[1,7]{1,0:T(1,128)}, u32[]{:S(2)}) copy-start(f32[1,7]{1,0:T(1,128)} %get-tuple-element.5) | copy-start | bytes 88

commit v3 on v2

--- a/solution.py
+++ b/solution.py
@@ -12,6 +12,7 @@
 LANES = 128
 ROWS = 8
 EARLY = 2
+HELD = 1
 
 
 def take_rows(values, rows):
@@ -69,11 +70,10 @@
     norm = 1.0 / (columns * devices * layers)
 
     barrier = pltpu.get_barrier_semaphore()
-    for step in range(1, devices):
-        peer = lax.rem(me + step, devices)
-        pl.semaphore_signal(
-            barrier, inc=1, device_id=(peer // groups, lax.rem(peer, groups)), device_id_type=MESH
-        )
+    others = [lax.rem(me + step, devices) for step in range(1, devices)]
+    peers = [(other // groups, lax.rem(other, groups)) for other in others]
+    for peer in peers:
+        pl.semaphore_signal(barrier, inc=1, device_id=peer, device_id_type=MESH)
 
     row = lax.broadcasted_iota(jnp.int32, (ROWS, LANES), 0)
     lane = lax.broadcasted_iota(jnp.int32, (1, LANES), 1)
@@ -149,8 +149,10 @@
                 def _():
                     pl.semaphore_wait(barrier, devices - 1)
 
-                for copy in early_copies(block, cs):
-                    copy.start()
+                @pl.when(block < columns // LANES - HELD)
+                def _():
+                    for copy in early_copies(block, cs):
+                        copy.start()
 
             return 0
 
@@ -167,22 +169,29 @@
     def to_column(values):
         return jnp.sum(jnp.where(t_row == t_lane, values, 0.0), axis=1, keepdims=True)
 
-    packed[...] = jnp.zeros_like(packed)
-    for kind in range(2):
-        packed[kind : kind + 1] = to_row(jnp.sum(part[kind], axis=1, keepdims=True), 0)
-    arrived[pl.ds(me, 1)] = packed[...][None]
-    sums = []
-    for step in range(1, devices):
-        peer = lax.rem(me + step, devices)
-        copy = pltpu.make_async_remote_copy(
-            src_ref=packed, dst_ref=arrived.at[me], send_sem=sum_send.at[step - 1], recv_sem=sum_recv.at[step - 1],
-            device_id=(peer // groups, lax.rem(peer, groups)), device_id_type=MESH,
-        )
-        copy.start()
-        sums.append(copy)
-    for copy in sums:
-        copy.wait()
-    total = jnp.sum(arrived[...], axis=0) * norm
+
+    def share(values, source, slots, slot, peers, send_sem, recv_sem):
+        source[...] = values
+        slots[pl.ds(slot, 1)] = values[None]
+        sums = []
+        for i, peer in enumerate(peers):
+            copy = pltpu.make_async_remote_copy(
+                src_ref=source, dst_ref=slots.at[slot], send_sem=send_sem.at[i],
+                recv_sem=recv_sem.at[i], device_id=peer, device_id_type=MESH,
+            )
+            copy.start()
+            sums.append(copy)
+        for block in range(columns // LANES - HELD, columns // LANES):
+            for copy in early_copies(block, pl.ds(block * LANES, LANES)):
+                copy.start()
+        for copy in sums:
+            copy.wait()
+        return jnp.sum(slots[...], axis=0)
+
+    mine = jnp.concatenate(
+        [to_row(jnp.sum(part[kind], axis=1, keepdims=True), 0) for kind in range(2)], axis=0
+    )
+    total = share(mine, packed, arrived, me, peers, sum_send, sum_recv) * norm
     before = to_column(total[0:1])
     after = to_column(total[1:2])
     ratio[...] = jnp.broadcast_to(before / after, (tracers, LANES))

time: 48.7 us -> 48.2 us (0.990)
    pallas_call x1, Pallas kernels: 44.2 us -> 43.8 us  [per_device(): pl.pallas_call(functools.partial(kernel, cols, groups), out_shape=(jax.Sh...]
where the time goes in v3:
time: 48.2 us; the launch traced here: 48 us
  Pallas kernels  43.8 us (91%)
  local copies, waits for them, and re-layouts  3.65 us (8%)
  between operations  0.65 us (1%)
    pallas_call x1, Pallas kernels, per_device(): pl.pallas_call(functools.partial(kernel, cols, groups), out_shape=(jax.Sh...  43.8 us
    unnamed x4, local copies, waits for them, and re-layouts  3.65 us

profile of v3, /device:TPU:0, one launch (start us, length us, event | category | flops | bytes accessed | tf_op | source)
XLA Modules:
  0.0 48.0 jit_solution(14271464513312234073)
XLA Ops:
  0.6 43.8 %remap_fix_exchange.1 = (bf16[7,72,2048]{2,1,0:T(8,128)(2,1)}, f32[1,7]{1,0:T(1,128)}) custom-call(bf16[28,127,512]{2,1,0:T(8,128)(2,1)} %x_ref.1, f32[127,512]{1,0:T(8,128)} %dp_ref.1, f32[71,512]{1,0:T(8,128)} %cut_ref.1, s32[2,72,512]{2,1,0:T(8,128)} %bounds_ref.1), custom_call_target="tpu_custom_call" | custom-call | tf_op jit(solution)/shard_map/remap_fix_exchange/pallas_call | solution.py:247
  44.4 0.0 copy-start
  44.4 3.1 %copy.8 = bf16[7,72,2048]{2,1,0:T(8,128)(2,1)} copy(bf16[7,72,2048]{2,1,0:T(8,128)(2,1)} %get-tuple-element.8) | data formatting | bytes 4128768
  47.5 0.0 copy-done
  47.5 0.5 %copy.9 = f32[7]{0:T(128)} copy(f32[7]{0:T(128)S(1)} %bitcast.1) | data formatting | bytes 56
Async XLA Ops:
  44.4 3.1 %copy-start = (f32[1,7]{1,0:T(1,128)S(1)}, f32[1,7]{1,0:T(1,128)}, u32[]{:S(2)}) copy-start(f32[1,7]{1,0:T(1,128)} %get-tuple-element.5) | copy-start | bytes 88
